TPU v7x, 32 devices: a whole 2x2x4 slice. The times are simulated.
32 devices in a mesh: lat: 4 (over y, core), lon: 8 (over z, x).
Axes of the slice: x: 2, y: 2, z: 4, core: 2. Of those that a mesh axis runs over, the one named last changes fastest.
Arguments:
- ensemble: bfloat16 [32, 128, 2048], P('lat', 'lon'), may hold values from -6 to 6
- channel_weights: bfloat16 [4, 8, 32, 32, 128], P('lat', 'lon'), may hold values from -1 to 1
- block_column: int32 [4, 8, 32], P('lat', 'lon'), may hold values from 0 to 127
- innovation: bfloat16 [4, 8, 32, 128], P('lat', 'lon'), may hold values from -6 to 6
- error_precision: bfloat16 [4, 8, 32, 128], P('lat', 'lon'), may hold values from 0.25 to 4
- block_count: int32 [4, 8], P('lat', 'lon'), may hold values from 1 to 32, as said below
- neighbours: int32 [16, 64, 12], P('lat', 'lon'), may hold values from 0 to 287
Outputs:
- analysis: bfloat16 [32, 128, 2048], P('lat', 'lon')
Inputs may be any that keep to these rules, and one draw needn't show every extreme that they name: The live blocks of a tile are its first block_count slots; at least one tile fills all 32 slots.
All inputs are finite; a program needn't handle non-finite values.
Results may differ from a plain program's by a relative error of at most 0.0074.
Values may be sent and summed in bfloat16 or wider, within the bound.
No kernel may reach another device: no remote copies, remote signals or barrier semaphores. Data moves between devices by JAX's collectives and lax.ppermute only.
A program may use at most 64 MiB of HBM per device.

v0:
```python
import jax
import jax.numpy as jnp
from jax import lax
from jax.sharding import PartitionSpec as P

NSI = 6
LOC = 12


def padded(block, sides, width, periodic):
    for axis, dim in sides:
        count = lax.axis_size(axis)
        forward = [(i, i + 1) for i in range(count - 1)]
        if periodic:
            forward.append((count - 1, 0))
        backward = [(target, source) for source, target in forward]
        low = lax.ppermute(
            lax.slice_in_dim(block, block.shape[dim] - width, None, axis=dim), axis, forward
        )
        high = lax.ppermute(lax.slice_in_dim(block, 0, width, axis=dim), axis, backward)
        block = jnp.concatenate([low, block, high], axis=dim)
    return block


def from_behind(block, axis, distance):
    devices = range(lax.axis_size(axis))
    route = [(i - distance, i) for i in devices if i - distance in devices]
    return lax.ppermute(block, axis, route)


def passed_along(value, axis, steps):
    count = lax.axis_size(axis)
    pairs = [(source, (source + steps) % count) for source in range(count)]
    return lax.ppermute(value, axis, pairs)


def newton_schulz(gram_matrix, projected):
    members = gram_matrix.shape[-1]
    identity = jnp.eye(members, dtype=jnp.float32)
    frobenius = jnp.sqrt(jnp.sum(gram_matrix * gram_matrix, axis=(1, 2)))
    current = gram_matrix / frobenius[:, None, None]
    inverse = jnp.broadcast_to(identity, gram_matrix.shape)
    for turn_index in range(NSI):
        middle = 1.5 * identity - 0.5 * jnp.einsum(
            "pij,pjk->pik", inverse, current, precision=lax.Precision.HIGHEST
        )
        current = jnp.einsum("pij,pjk->pik", current, middle, precision=lax.Precision.HIGHEST)
        inverse = jnp.einsum("pij,pjk->pik", middle, inverse, precision=lax.Precision.HIGHEST)
    root_scale = jnp.sqrt(frobenius)
    spread_part = inverse * (jnp.sqrt(jnp.float32(members - 1.0)) / root_scale)[:, None, None]
    halfway = jnp.einsum("pij,pj->pi", inverse, projected, precision=lax.Precision.HIGHEST)
    mean_shift = (
        jnp.einsum("pij,pj->pi", inverse, halfway, precision=lax.Precision.HIGHEST)
        / frobenius[:, None]
    )
    return (spread_part + mean_shift[:, :, None]).astype(jnp.bfloat16)


def body(
    ensemble, channel_weights, block_column, innovation, error_precision, block_count, neighbours
):
    lat_rows, lon_cols, row_width = ensemble.shape
    slot_count = block_column.shape[2]
    levels = channel_weights.shape[3]
    block_len = channel_weights.shape[4]
    members = row_width // levels
    coarse_lat = neighbours.shape[0]
    coarse_lon = neighbours.shape[1]
    columns = block_column[0, 0]
    state_cols = ensemble.reshape(lat_rows * lon_cols, levels, members)
    picked = state_cols[columns].astype(jnp.float32)
    average = jnp.mean(picked, axis=2, keepdims=True)
    anomaly = (picked - average).astype(jnp.bfloat16)
    blocks = jnp.einsum(
        "blk,blo->bko", anomaly, channel_weights[0, 0], preferred_element_type=jnp.float32
    ).astype(jnp.bfloat16)
    live_mask = (jnp.arange(slot_count, dtype=jnp.int32) < block_count[0, 0]).astype(jnp.bfloat16)
    weighted = error_precision[0, 0] * live_mask[:, None]
    position = jnp.stack(
        [(columns // lon_cols).astype(jnp.bfloat16), (columns % lon_cols).astype(jnp.bfloat16)], 1
    )
    position_row = jnp.concatenate(
        [position, jnp.zeros((slot_count, block_len - 2), jnp.bfloat16)], 1
    )
    facts = jnp.stack([innovation[0, 0], weighted, position_row], 1)
    packed = jnp.concatenate([blocks, facts], 1)[None, None]
    packed = padded(packed, (("lat", 0),), 1, False)
    packed = padded(packed, (("lon", 1),), 1, True)
    flat_packed = packed.reshape(9 * slot_count, members + 3, block_len)
    flat_blocks = flat_packed[:, :members]
    flat_facts = flat_packed[:, members:].astype(jnp.float32)
    offset = jnp.arange(9 * slot_count, dtype=jnp.int32) // slot_count
    north_south = (offset // 3 - 1).astype(jnp.float32) * lat_rows + flat_facts[:, 2, 0]
    east_west = (offset % 3 - 1).astype(jnp.float32) * lon_cols + flat_facts[:, 2, 1]
    point_cols = 2.0 * jnp.arange(coarse_lon, dtype=jnp.int32).astype(jnp.float32)[:, None]

    def coarse_row(pieces):
        row_index, listed = pieces
        chosen = flat_blocks[listed]
        delta_lat = north_south[listed] - 2.0 * row_index.astype(jnp.float32)
        delta_lon = east_west[listed] - point_cols
        taper = jnp.exp(-(delta_lat * delta_lat + delta_lon * delta_lon) / (2.0 * LOC * LOC))
        root_weight = jnp.sqrt(taper[:, :, None] * flat_facts[listed, 1])
        scaled = (root_weight[:, :, None, :] * chosen).astype(jnp.bfloat16)
        forced = (root_weight * flat_facts[listed, 0]).astype(jnp.bfloat16)
        gram_matrix = jnp.einsum(
            "pjko,pjlo->pkl", scaled, scaled, preferred_element_type=jnp.float32
        ) + (members - 1.0) * jnp.eye(members, dtype=jnp.float32)
        projected = jnp.einsum("pjko,pjo->pk", scaled, forced, preferred_element_type=jnp.float32)
        return newton_schulz(gram_matrix, projected)

    coarse = lax.map(coarse_row, (jnp.arange(coarse_lat, dtype=jnp.int32), neighbours))
    coarse_flat = coarse.reshape(coarse_lat, coarse_lon, members * members)
    below = from_behind(coarse_flat[:1], "lat", -1)
    ending = lax.axis_index("lat") == lax.axis_size("lat") - 1
    below = jnp.where(ending, coarse_flat[-1:], below)
    extended = jnp.concatenate([coarse_flat, below], 0)
    beside = passed_along(extended[:, :1], "lon", -1)
    coarse_ext = jnp.concatenate([extended, beside], 1).astype(jnp.float32)
    row_even = coarse_ext[:-1]
    row_odd = 0.5 * (coarse_ext[:-1] + coarse_ext[1:])
    fine_rows = jnp.stack([row_even, row_odd], 1).reshape(
        lat_rows, coarse_lon + 1, members * members
    )
    col_even = fine_rows[:, :-1]
    col_odd = 0.5 * (fine_rows[:, :-1] + fine_rows[:, 1:])
    blended = (
        jnp.stack([col_even, col_odd], 2)
        .reshape(lat_rows, lon_cols, members, members)
        .astype(jnp.bfloat16)
    )
    state_full = ensemble.reshape(lat_rows, lon_cols, levels, members).astype(jnp.float32)
    center = jnp.mean(state_full, axis=3, keepdims=True)
    spread = (state_full - center).astype(jnp.bfloat16)
    result = center + jnp.einsum(
        "rclk,rckj->rclj", spread, blended, preferred_element_type=jnp.float32
    )
    return result.astype(jnp.bfloat16).reshape(lat_rows, lon_cols, row_width)


def solution(mesh):
    return jax.shard_map(
        body,
        mesh=mesh,
        in_specs=(
            P("lat", "lon", None),
            P("lat", "lon", None, None, None),
            P("lat", "lon", None),
            P("lat", "lon", None, None),
            P("lat", "lon", None, None),
            P("lat", "lon"),
            P("lat", "lon", None),
        ),
        out_specs=P("lat", "lon", None),
        check_vma=False,
    )
```

profile of v0, /device:TPU:1, one launch (start us, length us, event | category | flops | bytes accessed | tf_op | source)
XLA Modules:
  0.0 207.3 jit_solution(13619992651995787870)
XLA Ops:
  0.7 2.1 reshape.291
  5.7 4.5 %collective-permute-start = (bf16[1,1,32,67,128]{4,2,3,1,0:T(8,128)(2,1)S(1)}, bf16[1,1,32,67,128]{4,2,3,1,0:T(8,128)(2,1)S(1)}, u32[]{:S(2)}, u32[]{:S(2)}) collective-permute-start(bf16[1,1,32,67,128]{4,2,3,1,0:T(8,128)(2,1)S(1)} %copy.30), channel_id=1, source_target_pairs={{0,8},{8,16},{16,24},{1,9},{9,17},{17,25},{2,10},{10,18},{18,26},{... | collective-permute-start | bytes 1646600 | tf_op jit(solution)/shard_map/ppermute | solution.py:17
  10.3 1.9 collective-permute-start.1
  12.2 4.4 %collective-permute-done = bf16[1,1,32,67,128]{4,2,3,1,0:T(8,128)(2,1)S(1)} collective-permute-done((bf16[1,1,32,67,128]{4,2,3,1,0:T(8,128)(2,1)S(1)}, bf16[1,1,32,67,128]{4,2,3,1,0:T(8,128)(2,1)S(1)}, u32[]{:S(2)}, u32[]{:S(2)}) %collective-permute-start) | collective-permute-done | bytes 548896 | tf_op jit(solution)/shard_map/ppermute | solution.py:17
  16.9 4.6 %collective-permute-done.1 = bf16[1,1,32,67,128]{4,2,3,1,0:T(8,128)(2,1)S(1)} collective-permute-done((bf16[1,1,32,67,128]{4,2,3,1,0:T(8,128)(2,1)S(1)}, bf16[1,1,32,67,128]{4,2,3,1,0:T(8,128)(2,1)S(1)}, u32[]{:S(2)}, u32[]{:S(2)}) %collective-permute-start.1) | collective-permute-done | bytes 548896 | tf_op jit(solution)/shard_map/ppermute | solution.py:20
  21.9 1.4 copy.34
  23.3 1.2 collective-permute-start.2
  24.5 3.0 %collective-permute-start.3 = (bf16[3,1,32,67,128]{4,2,3,1,0:T(8,128)(2,1)}, bf16[3,1,32,67,128]{4,2,3,1,0:T(8,128)(2,1)}, u32[]{:S(2)}, u32[]{:S(2)}) collective-permute-start(bf16[3,1,32,67,128]{4,2,3,1,0:T(8,128)(2,1)} %copy.34), channel_id=1, source_target_pairs={{1,0},{2,1},{3,2},{4,3},{5,4},{6,5},{7,6},{0,7},{9,8},{10,9},{11,1... | collective-permute-start | bytes 4939784 | tf_op jit(solution)/shard_map/ppermute | solution.py:20
  27.6 61.5 %collective-permute-done.2 = bf16[3,1,32,67,128]{4,2,3,1,0:T(8,128)(2,1)} collective-permute-done((bf16[3,1,32,67,128]{4,2,3,1,0:T(8,128)(2,1)}, bf16[3,1,32,67,128]{4,2,3,1,0:T(8,128)(2,1)}, u32[]{:S(2)}, u32[]{:S(2)}) %collective-permute-start.2) | collective-permute-done | bytes 1646624 | tf_op jit(solution)/shard_map/ppermute | solution.py:17
  89.1 2.1 %copy.36 = bf16[3,1,32,67,128]{4,3,2,1,0:T(8,128)(2,1)S(1)} copy(bf16[3,1,32,67,128]{4,2,3,1,0:T(8,128)(2,1)} %collective-permute-done.2) | data formatting | bytes 3293184 | tf_op jit(solution)/shard_map/ppermute | solution.py:17
  91.2 2.1 %copy.37 = bf16[3,1,32,67,128]{4,3,2,1,0:T(8,128)(2,1)S(1)} copy(bf16[3,1,32,67,128]{4,2,3,1,0:T(8,128)(2,1)} %collective-permute-done.3) | data formatting | bytes 3293184 | tf_op jit(solution)/shard_map/ppermute | solution.py:20
  93.3 1.7 pad_maximum_fusion
  95.1 3.5 %slice.69 = bf16[288,64,128]{2,1,0:T(8,128)(2,1)} slice(bf16[288,67,128]{2,1,0:T(8,128)(2,1)S(1)} %bitcast.213), slice={[0:288], [0:64], [0:128]} | slice | bytes 9437184 | tf_op jit(solution)/shard_map/slice | solution.py:90
  98.7 2.9 %slice_reduce_fusion = (f32[288]{0:T(512)S(1)}, f32[288]{0:T(512)S(1)}) fusion(f32[288,3,128]{2,1,0:T(4,128)S(1)} %slice_convert_fusion.1), kind=kLoop, calls=%fused_computation.79 | loop fusion | bytes 4608 | tf_op jit(solution)/shard_map/slice | solution.py:94
  101.6 82.6 %while.11 = (s32[]{:T(128)}, bf16[4,8,64,64]{3,2,1,0:T(8,128)(2,1)S(1)}, s32[4,8,12]{2,1,0:T(8,128)}, f32[288]{0:T(512)S(1)}, s32[4]{0:T(128)S(1)}, /*index=5*/f...) while((s32[]{:T(128)}, ...), condition=%wide.region_4.5_spmd.clone, body=%wide.region_2.4_spmd.clone.sunk | while | flops 536280000 | bytes 14421297 | solution.py:112
  102.6 1.3 gather_fusion.3
  105.2 1.3 gather_fusion.4
  106.8 1.4 gather_fusion.2
  108.2 1.4 gather_fusion.1
  109.7 3.2 %gather_fusion = bf16[96,64,128]{2,1,0:T(8,128)(2,1)S(1)} fusion(bf16[288,64,128]{2,1,0:T(8,128)(2,1)} %get-tuple-element.222, s32[1024]{0:T(1024)S(1)} %pad_clamp_fusion.3), kind=kCustom, calls=%fused_computation.3.clone.clone.1 | custom fusion | bytes 3146112 | tf_op jit(solution)/shard_map/while/body/eval_jaxpr/gather | solution.py:99
  112.9 0.8 multiply_reduce_fusion.2
  123.2 1.3 gather_fusion.3
  125.8 1.3 gather_fusion.4
  127.4 1.4 gather_fusion.2
  128.8 1.4 gather_fusion.1
  130.3 3.2 %gather_fusion = bf16[96,64,128]{2,1,0:T(8,128)(2,1)S(1)} fusion(bf16[288,64,128]{2,1,0:T(8,128)(2,1)} %get-tuple-element.222, s32[1024]{0:T(1024)S(1)} %pad_clamp_fusion.3), kind=kCustom, calls=%fused_computation.3.clone.clone.1 | custom fusion | bytes 3146112 | tf_op jit(solution)/shard_map/while/body/eval_jaxpr/gather | solution.py:99
  133.5 0.8 multiply_reduce_fusion.2
  143.8 1.3 gather_fusion.3
  146.5 1.3 gather_fusion.4
  148.0 1.4 gather_fusion.2
  149.5 1.4 gather_fusion.1
  150.9 3.2 %gather_fusion = bf16[96,64,128]{2,1,0:T(8,128)(2,1)S(1)} fusion(bf16[288,64,128]{2,1,0:T(8,128)(2,1)} %get-tuple-element.222, s32[1024]{0:T(1024)S(1)} %pad_clamp_fusion.3), kind=kCustom, calls=%fused_computation.3.clone.clone.1 | custom fusion | bytes 3146112 | tf_op jit(solution)/shard_map/while/body/eval_jaxpr/gather | solution.py:99
  164.5 1.3 gather_fusion.3
  167.1 1.3 gather_fusion.4
  168.6 1.4 gather_fusion.2
  170.1 1.4 gather_fusion.1
  171.5 3.2 %gather_fusion = bf16[96,64,128]{2,1,0:T(8,128)(2,1)S(1)} fusion(bf16[288,64,128]{2,1,0:T(8,128)(2,1)} %get-tuple-element.222, s32[1024]{0:T(1024)S(1)} %pad_clamp_fusion.3), kind=kCustom, calls=%fused_computation.3.clone.clone.1 | custom fusion | bytes 3146112 | tf_op jit(solution)/shard_map/while/body/eval_jaxpr/gather | solution.py:99
  184.3 0.8 slice.48
  185.1 2.1 %collective-permute-start.4 = (bf16[1,8,4096]{2,1,0:T(8,128)(2,1)}, bf16[1,8,4096]{2,1,0:T(8,128)(2,1)}, u32[]{:S(2)}, u32[]{:S(2)}) collective-permute-start(bf16[1,8,4096]{2,1,0:T(8,128)(2,1)} %slice.48), channel_id=1, source_target_pairs={{8,0},{16,8},{24,16},{9,1},{17,9},{25,17},{10,2},{18,10},{26,18},{... | collective-permute-start | bytes 196616 | tf_op jit(solution)/shard_map/ppermute | solution.py:28
  187.3 0.9 reshape.296
  189.5 1.5 collective-permute-done.4
  191.0 0.8 broadcast_select_fusion
  191.9 4.9 %collective-permute-start.5 = (bf16[5,1,4096]{2,1,0:T(2,128)(2,1)S(1)}, bf16[5,1,4096]{2,1,0:T(2,128)(2,1)S(1)}, u32[]{:S(2)}, u32[]{:S(2)}) collective-permute-start(bf16[5,1,4096]{2,1,0:T(2,128)(2,1)S(1)} %pad_maximum_fusion.4), channel_id=1, source_target_pairs={{0,7},{1,0},{2,1},{3,2},{4,3},{5,4},{6,5},{7,6},{8,15},{9,8},{10,9... | collective-permute-start | bytes 122888 | tf_op jit(solution)/shard_map/ppermute | solution.py:34
  196.8 1.5 collective-permute-done.5
  199.1 1.1 copy.40
  200.2 2.4 %convert_element_type.110 = bf16[8,16,64,64]{3,2,1,0:T(8,128)(2,1)} reshape(bf16[8,8,2,4096]{3,2,1,0:T(2,128)(2,1)S(1)} %copy.40) | data formatting | bytes 2097152 | tf_op jit(solution)/shard_map/convert_element_type | solution.py:130
  202.6 3.1 %add_convert_fusion.1 = bf16[8,16,32,64]{3,2,1,0:T(8,128)(2,1)S(1)} fusion(bf16[8,16,64,64]{3,2,1,0:T(8,128)(2,1)} %convert_element_type.110, f32[8,16,32,64]{3,2,1,0:T(8,128)S(1)} %reshape.296, f32[8,16,32]{2,1,0:T(8,128)S(1)} %broadcast_multiply_fusion), kind=kOutput, calls=%fused_computation.55 | convolution fusion | flops 34603008 | bytes 2637824 | tf_op jit(solution)/shard_map/rclk,rckj->rclj/dot_general | solution.py:135
  205.7 1.6 reshape.295
  (212 shorter events, 49.4 us)
Async XLA Ops:
  0.0 4.7 %copy-start = (bf16[1,1,32,32,128]{4,3,2,1,0:T(8,128)(2,1)S(1)}, bf16[1,1,32,32,128]{4,3,2,1,0:T(8,128)(2,1)}, u32[]{:S(2)}) copy-start(bf16[1,1,32,32,128]{4,3,2,1,0:T(8,128)(2,1)} %param.10) | copy-start | bytes 786436
  0.0 4.7 %copy-start.2 = (bf16[1,1,32,128]{3,2,1,0:T(8,128)(2,1)S(1)}, bf16[1,1,32,128]{3,2,1,0:T(8,128)(2,1)}, u32[]{:S(2)}) copy-start(bf16[1,1,32,128]{3,2,1,0:T(8,128)(2,1)} %param.12) | copy-start | bytes 24580
  0.7 4.7 %copy-start.3 = (bf16[1,1,32,128]{3,2,1,0:T(8,128)(2,1)S(1)}, bf16[1,1,32,128]{3,2,1,0:T(8,128)(2,1)}, u32[]{:S(2)}) copy-start(bf16[1,1,32,128]{3,2,1,0:T(8,128)(2,1)} %param.13) | copy-start | bytes 24580
  5.7 10.9 %collective-permute-start = (bf16[1,1,32,67,128]{4,2,3,1,0:T(8,128)(2,1)S(1)}, bf16[1,1,32,67,128]{4,2,3,1,0:T(8,128)(2,1)S(1)}, u32[]{:S(2)}, u32[]{:S(2)}) collective-permute-start(bf16[1,1,32,67,128]{4,2,3,1,0:T(8,128)(2,1)S(1)} %copy.30), channel_id=1, source_target_pairs={{0,8},{8,16},{16,24},{1,9},{9,17},{17,25},{2,10},{10,18},{18,26},{... | collective-permute-start | bytes 1646600 | tf_op jit(solution)/shard_map/ppermute | solution.py:17
  10.3 11.2 %collective-permute-start.1 = (bf16[1,1,32,67,128]{4,2,3,1,0:T(8,128)(2,1)S(1)}, bf16[1,1,32,67,128]{4,2,3,1,0:T(8,128)(2,1)S(1)}, u32[]{:S(2)}, u32[]{:S(2)}) collective-permute-start(bf16[1,1,32,67,128]{4,2,3,1,0:T(8,128)(2,1)S(1)} %copy.30), channel_id=1, source_target_pairs={{8,0},{16,8},{24,16},{9,1},{17,9},{25,17},{10,2},{18,10},{26,18},{... | collective-permute-start | bytes 1646600 | tf_op jit(solution)/shard_map/ppermute | solution.py:20
  23.3 65.8 %collective-permute-start.2 = (bf16[3,1,32,67,128]{4,2,3,1,0:T(8,128)(2,1)}, bf16[3,1,32,67,128]{4,2,3,1,0:T(8,128)(2,1)}, u32[]{:S(2)}, u32[]{:S(2)}) collective-permute-start(bf16[3,1,32,67,128]{4,2,3,1,0:T(8,128)(2,1)} %copy.34), channel_id=1, source_target_pairs={{0,1},{1,2},{2,3},{3,4},{4,5},{5,6},{6,7},{7,0},{8,9},{9,10},{10,1... | collective-permute-start | bytes 4939784 | tf_op jit(solution)/shard_map/ppermute | solution.py:17
  24.5 66.7 %collective-permute-start.3 = (bf16[3,1,32,67,128]{4,2,3,1,0:T(8,128)(2,1)}, bf16[3,1,32,67,128]{4,2,3,1,0:T(8,128)(2,1)}, u32[]{:S(2)}, u32[]{:S(2)}) collective-permute-start(bf16[3,1,32,67,128]{4,2,3,1,0:T(8,128)(2,1)} %copy.34), channel_id=1, source_target_pairs={{1,0},{2,1},{3,2},{4,3},{5,4},{6,5},{7,6},{0,7},{9,8},{10,9},{11,1... | collective-permute-start | bytes 4939784 | tf_op jit(solution)/shard_map/ppermute | solution.py:20
  101.6 85.6 %copy-start.1 = (bf16[8,16,2048]{2,1,0:T(8,128)(2,1)S(1)}, bf16[8,16,2048]{2,1,0:T(8,128)(2,1)}, u32[]{:S(2)}) copy-start(bf16[8,16,2048]{2,1,0:T(8,128)(2,1)} %param.9) | copy-start | bytes 1572868
  185.1 5.9 %collective-permute-start.4 = (bf16[1,8,4096]{2,1,0:T(8,128)(2,1)}, bf16[1,8,4096]{2,1,0:T(8,128)(2,1)}, u32[]{:S(2)}, u32[]{:S(2)}) collective-permute-start(bf16[1,8,4096]{2,1,0:T(8,128)(2,1)} %slice.48), channel_id=1, source_target_pairs={{8,0},{16,8},{24,16},{9,1},{17,9},{25,17},{10,2},{18,10},{26,18},{... | collective-permute-start | bytes 196616 | tf_op jit(solution)/shard_map/ppermute | solution.py:28
  191.9 6.4 %collective-permute-start.5 = (bf16[5,1,4096]{2,1,0:T(2,128)(2,1)S(1)}, bf16[5,1,4096]{2,1,0:T(2,128)(2,1)S(1)}, u32[]{:S(2)}, u32[]{:S(2)}) collective-permute-start(bf16[5,1,4096]{2,1,0:T(2,128)(2,1)S(1)} %pad_maximum_fusion.4), channel_id=1, source_target_pairs={{0,7},{1,0},{2,1},{3,2},{4,3},{5,4},{6,5},{7,6},{8,15},{9,8},{10,9... | collective-permute-start | bytes 122888 | tf_op jit(solution)/shard_map/ppermute | solution.py:34
where the time goes:
time: 208 us; the launch traced here: 207 us
  waiting for transfers between devices  73.6 us (35%)
  local copies, waits for them, and re-layouts  60.9 us (29%)
  matrix products  40 us (19%)
  starting transfers between devices  17.8 us (9%)
  other arithmetic  10.3 us (5%)
  loops' own time  3.75 us (2%)
    ppermute x2, waiting for transfers between devices, padded(): lax.ppermute(lax.slice_in_dim(block, block.shape[dim] - width, None, axis...  65.9 us
    gather x4, local copies, waits for them, and re-layouts, coarse_row(): chosen = flat_blocks[listed]  12.7 us
    dot_general x24, matrix products, newton_schulz(): jnp.einsum('pij,pjk->pik', inverse, current, precision=lax.Precision.HIGH...  9.58 us
    dot_general x24, matrix products, newton_schulz(): jnp.einsum('pij,pjk->pik', middle, inverse, precision=lax.Precision.HIGHEST)  9.21 us
    dot_general x20, matrix products, newton_schulz(): jnp.einsum('pij,pjk->pik', current, middle, precision=lax.Precision.HIGHEST)  7.98 us
    ppermute x2, starting transfers between devices, padded(): lax.ppermute(lax.slice_in_dim(block, block.shape[dim] - width, None, axis...  5.74 us
    gather x8, local copies, waits for them, and re-layouts, coarse_row(): root_weight = jnp.sqrt(taper[:, :, None] * flat_facts[listed, 1])  5.46 us
    gather x8, local copies, waits for them, and re-layouts, coarse_row(): forced = (root_weight * flat_facts[listed, 0]).astype(jnp.bfloat16)  5.43 us
  transfers between devices with their start and end apart: 6, of which 6 were waited for; matrix products, arithmetic and copies ran while one was open for 2% of the time, Pallas kernels for 0%

commit v1 on v0

v1 whole, which is shorter than its diff:
```python
import functools
import math

import jax
import jax.numpy as jnp
import numpy as np
from jax import lax
from jax.experimental import pallas as pl
from jax.experimental.pallas import tpu as pltpu
from jax.sharding import PartitionSpec as P

NSI = 6
LOC = 12
F32 = jnp.float32
BF16 = jnp.bfloat16
VMEM = pl.BlockSpec(memory_space=pltpu.VMEM)
SMEM = pl.BlockSpec(memory_space=pltpu.SMEM)
ANY = pl.BlockSpec(memory_space=pl.ANY)
NT = (((1,), (1,)), ((), ()))


def ring(axis, step, periodic):
    n = lax.axis_size(axis)
    pairs = [(s, s + step) for s in range(n)]
    if periodic:
        return [(s, t % n) for s, t in pairs]
    return [(s, t) for s, t in pairs if 0 <= t < n]


def lane_iota(shape):
    return lax.broadcasted_iota(jnp.int32, shape, len(shape) - 1)


def row_iota(shape):
    return lax.broadcasted_iota(jnp.int32, shape, len(shape) - 2)


def mm(a, b):
    return jnp.dot(a, b, preferred_element_type=F32)


def split(x):
    hi = x.astype(BF16)
    return hi, (x - hi.astype(F32)).astype(BF16)


def prepare_kernel(dims, col_ref, count_ref, ens_ref, w_ref, inn_ref, prec_ref, colrow_ref,
                   anom_ref, cent_ref, pack_ref, x_ref, wf_ref):
    rows, cols, members, levels, slots, obs = dims
    pieces = levels // 2
    wide = 2 * members
    for r in range(rows):
        for t in range(pieces):
            x = ens_ref[r, :, t * wide:(t + 1) * wide].astype(F32)
            x_ref[pl.ds(r * cols * pieces + t, cols, stride=pieces), :] = x
    same = (row_iota((wide, wide)) < members) == (lane_iota((wide, wide)) < members)
    averaging = jnp.where(same, 1.0 / members, 0.0).astype(BF16)
    step = cols * pieces
    for r in range(rows):
        x = x_ref[r * step:(r + 1) * step, :]
        c = mm(x.astype(BF16), averaging)
        cent_ref[r * step:(r + 1) * step, :] = c
        anom_ref[r * step:(r + 1) * step, :] = (x - c).astype(BF16)
    wf_ref[...] = w_ref[...].astype(F32)
    group = wide // pieces
    empty = jnp.zeros((pieces, obs), BF16)
    for first in range(0, slots, group):
        picked = [
            anom_ref[pl.ds(pl.multiple_of(col_ref[first + b] * pieces, pieces), pieces), :]
            for b in range(group)
        ]
        turned = jnp.concatenate(picked, 0).astype(F32).T.astype(BF16)
        left = jnp.concatenate([turned[:members], turned[members:]], 1)
        for b in range(group):
            right = []
            for half in range(2):
                part = wf_ref[pl.ds((first + b) * levels + half, pieces, stride=2), :].astype(BF16)
                right += [part if other == b else empty for other in range(group)]
            pack_ref[(first + b) * members:(first + b + 1) * members, :] = mm(
                left, jnp.concatenate(right, 0)).astype(BF16)
    base = slots * members
    pack_ref[base:base + slots, :] = inn_ref[...]
    live = row_iota((slots, obs)) < count_ref[0]
    weighted = jnp.where(live, prec_ref[...].astype(F32), 0.0)
    pack_ref[base + slots:base + 2 * slots, :] = weighted.astype(BF16)
    pack_ref[base + 2 * slots:, :] = colrow_ref[...]


def gram_kernel(dims, targets, place, base_ref, inrow_ref, hot_ref, low_ref, own_ref, high_ref,
                out_ref, buf_ref, inn_ref, root_ref, s_ref, sems):
    rows, cols, members, slots, obs, entries, size, points, lines = dims
    wide = 2 * members
    copies = [
        pltpu.make_async_copy(src, buf_ref.at[pl.ds(t * size, size), :], sems.at[t])
        for t, src in enumerate((low_ref, own_ref, high_ref))
    ]
    for c in copies:
        c.start()
    for c in copies:
        c.wait()
    base = slots * members
    lane1 = lane_iota((1, obs))
    where_col = jnp.zeros((1, obs), F32)
    where_u = jnp.zeros((1, obs), F32)
    spans = []
    for t in range(3):
        inn_ref[t * slots:(t + 1) * slots, :] = buf_ref[
            t * size + base:t * size + base + slots, :].astype(F32)
        spans.append(buf_ref[
            t * size + base + slots:t * size + base + 2 * slots, :].astype(F32))
        here = (lane1 >= t * slots) & (lane1 < (t + 1) * slots)
        line = buf_ref[t * size + base + 2 * slots:(t + 1) * size, :].astype(F32)[:1]
        where_col = jnp.where(here, line, where_col)
        where_u = jnp.where(here, t - 1.0, where_u)
    spans.append(jnp.zeros((obs - 3 * slots, obs), F32))
    qhi, qlo = split(jnp.sqrt(jnp.concatenate(spans, 0)))
    right_hi = jnp.concatenate([qhi, qhi], 0)
    col_row = jnp.floor((where_col + 0.5) / cols)
    col_col = where_col - col_row * cols
    dlat = where_u * rows + col_row
    batch = wide // lines
    for k, d in enumerate(targets):
        for first in range(0, points, batch):
            pieces = []
            for p in range(first, first + batch):
                a, c = place[p]
                north = dlat - 2.0 * a
                east = col_col - (d * cols + 2.0 * c)
                taper = jnp.exp((north * north + east * east) * (-1.0 / (4.0 * LOC * LOC)))
                at = (k * points + p) * lines
                pieces.append(hot_ref[at:at + lines, :] * taper)
            shi, slo = split(jnp.concatenate(pieces, 0))
            at = (k * points + first) * lines
            root_ref[at:at + batch * lines, :] = (
                mm(jnp.concatenate([shi, slo], 1), right_hi) + mm(shi, qlo))
    sub = 16
    lane = lane_iota((members, wide))
    first_half = lane < members
    rr = row_iota((members, wide))
    cc = jnp.where(first_half, lane, lane - members)
    line_half = lane_iota((1, wide)) < members

    def fill(q, buffer):
        for pair in range(2):
            for n in range(entries):
                over = slice(n * obs, (n + 1) * obs)
                extras = []
                for m in range(2):
                    point = q * 4 + pair * 2 + m
                    root = root_ref[pl.ds(point * lines + n, 1), :]
                    at = pl.multiple_of(base_ref[point * entries + n], sub)
                    block = buf_ref[pl.ds(at, members), :].astype(F32)
                    s_ref[buffer, pair, m * members:(m + 1) * members, over] = (
                        block * root).astype(BF16)
                    extra = inn_ref[pl.ds(inrow_ref[point * entries + n], 1), :] * root
                    extras.append(jnp.broadcast_to(extra, (sub // 2, obs)))
                s_ref[buffer, pair, wide:, over] = jnp.concatenate(extras, 0).astype(BF16)

    def finish(q, buffer):
        found = [
            lax.dot_general(s_ref[buffer, pair], s_ref[buffer, pair, :wide], NT,
                            preferred_element_type=F32)
            for pair in range(2)
        ]
        x, y = [jnp.where(first_half, f[:members], f[members:wide]) for f in found]
        px, py = [
            jnp.where(line_half, f[wide:wide + 1], f[wide + sub // 2:wide + sub // 2 + 1])
            for f in found
        ]
        out_ref[q, :members, :] = jnp.where(rr <= cc, x, y)
        dy = jnp.sum(jnp.where(rr == cc, y, 0.0), axis=0, keepdims=True)
        out_ref[q, members:, :] = jnp.concatenate(
            [dy, px, py, jnp.zeros((5, wide), F32)], 0)

    quads = len(targets) * points // 4
    fill(0, 0)

    def two(i, carry):
        fill(2 * i + 1, 1)
        finish(2 * i, 0)
        fill(jnp.minimum(2 * i + 2, quads - 1), 0)
        finish(2 * i + 1, 1)
        return carry

    lax.fori_loop(0, quads // 2, two, 0)


def newton_kernel(members, left_ref, own_ref, right_ref, out_ref,
                  g_ref, pr_ref, sq_ref, z_ref, m_ref,
                  yh_ref, yl_ref, zh_ref, zl_ref, mh_ref, ml_ref):
    quads = own_ref.shape[0]
    wide = 2 * members
    lane = lane_iota((members, wide))
    first_half = lane < members
    rr = row_iota((members, wide))
    cc = jnp.where(first_half, lane, lane - members)
    eye = jnp.where(rr == cc, 1.0, 0.0)
    keep_lo = jnp.where(first_half, 1.0, 0.0).astype(BF16)
    keep_hi = jnp.where(first_half, 0.0, 1.0).astype(BF16)

    def bd(x):
        return jnp.concatenate([x * keep_lo, x * keep_hi], 0)

    def mm3(left, right):
        lhi, llo = left
        rhi, rlo = right
        return mm(jnp.concatenate([lhi, llo], 1), jnp.concatenate([rhi, rhi], 0)) + mm(lhi, rlo)

    for q in range(quads):
        total = left_ref[q] + own_ref[q] + right_ref[q]
        packed = total[:members]
        t = packed.T
        turned = jnp.concatenate([t[:members], t[members:]], 1)
        dy = total[members:members + 1]
        x = jnp.where(rr <= cc, packed, turned)
        y = jnp.where(rr > cc, packed, jnp.where(rr == cc, dy, turned))
        for k, z in enumerate((x, y)):
            z = z + (members - 1.0) * eye
            g_ref[2 * q + k] = z
            sq_ref[2 * q + k:2 * q + k + 1, :] = jnp.sum(z * z, axis=0, keepdims=True)
            pr_ref[2 * q + k:2 * q + k + 1, :] = total[members + 1 + k:members + 2 + k]
    same = (row_iota((wide, wide)) < members) == (lane_iota((wide, wide)) < members)
    ones = jnp.where(same, 1.0, 0.0).astype(BF16)
    sq = sq_ref[...]
    s1 = sq.astype(BF16)
    rest = sq - s1.astype(F32)
    s2, s3 = split(rest)
    frob = jnp.sqrt(mm(s1, ones) + mm(s2, ones) + mm(s3, ones))
    sq_ref[...] = frob

    pairs = range(2 * quads)

    def put(refs, k, value):
        for ref, part in zip(refs, split(value)):
            ref[k] = part

    def bds(refs, k):
        return tuple(bd(ref[k]) for ref in refs)

    def get(refs, k):
        return tuple(ref[k] for ref in refs)

    ys, zs, ms = (yh_ref, yl_ref), (zh_ref, zl_ref), (mh_ref, ml_ref)
    for k in pairs:
        a = g_ref[k] / sq_ref[k:k + 1, :]
        put(zs, k, 1.5 * eye - 0.5 * a)
        put(ys, k, a)
    for k in pairs:
        put(ys, k, mm3(get(zs, k), bds(ys, k)))
    for turn in range(1, NSI):
        for k in pairs:
            put(ms, k, 1.5 * eye - 0.5 * mm3(get(zs, k), bds(ys, k)))
        for k in pairs:
            if turn < NSI - 1:
                yb, zb = bds(ys, k), bds(zs, k)
                both = mm3(get(ms, k), tuple(jnp.concatenate([u, v], 1) for u, v in zip(yb, zb)))
                put(ys, k, both[:, :wide])
                put(zs, k, both[:, wide:])
            else:
                z = mm3(get(ms, k), bds(zs, k))
                z_ref[k] = z
                put(zs, k, z)
    for k in pairs:
        proj = jnp.broadcast_to(pr_ref[k:k + 1, :], (16, wide))
        m_ref[k:k + 1, :] = mm3(split(proj), bds(zs, k))[:1]
    for k in pairs:
        half = jnp.broadcast_to(m_ref[k:k + 1, :], (16, wide))
        pr_ref[k:k + 1, :] = mm3(split(half), bds(zs, k))[:1]
    frob = sq_ref[...]
    shift = (pr_ref[...] / frob).T
    scale = math.sqrt(members - 1.0) / jnp.sqrt(frob)
    for at in range(2 * quads):
        col = jnp.where(first_half, shift[:members, at:at + 1], shift[members:, at:at + 1])
        out_ref[at] = (z_ref[at] * scale[at:at + 1] + col).astype(BF16)


def analysis_kernel(dims, spot, last_ref, own_ref, below_ref, beside_ref, corner_ref, anom_ref,
                    cent_ref, out_ref, d_ref, y_ref):
    rows, cols, members, levels, glat, glon = dims
    wide = 2 * members
    pieces = levels // 2
    lane = lane_iota((members, wide))
    first_half = lane < members
    keep_lo = jnp.where(first_half, 1.0, 0.0).astype(BF16)
    keep_hi = jnp.where(first_half, 0.0, 1.0).astype(BF16)
    ending = last_ref[0] == 1

    def both(pair, half):
        x = pair.astype(F32)
        other = pltpu.roll(x, members, 1)
        return jnp.where(first_half == (half == 0), x, other)

    def own(g, h):
        pair, half = spot[(g, h)]
        return both(own_ref[pair], half)

    def beside(g):
        pair, half = spot[(g, 0)]
        index = 0 if g == 0 else pair - glon // 2 + 1
        return both(beside_ref[index], half)

    for g in range(glat):
        for h in range(glon):
            d_ref[g * (glon + 1) + h] = own(g, h)
        d_ref[g * (glon + 1) + glon] = beside(g)
    for h in range(glon):
        d_ref[glat * (glon + 1) + h] = jnp.where(
            ending, own(glat - 1, h), both(below_ref[h // 2], h % 2))
    d_ref[glat * (glon + 1) + glon] = jnp.where(
        ending, beside(glat - 1), both(corner_ref[0], 0))

    def pair_of_rows(g, carry):
        for odd in range(2):
            r = 2 * g + odd
            line = []
            for h in range(glon + 1):
                t = d_ref[g * (glon + 1) + h]
                if odd:
                    t = 0.5 * (t + d_ref[(g + 1) * (glon + 1) + h])
                line.append(t)
            for c in range(cols):
                b = line[c // 2]
                if c % 2:
                    b = 0.5 * (b + line[c // 2 + 1])
                b = b.astype(BF16)
                b = jnp.concatenate([b * keep_lo, b * keep_hi], 0)
                at = pl.multiple_of((r * cols + c) * pieces, pieces)
                y_ref[c * pieces:(c + 1) * pieces, :] = (
                    cent_ref[pl.ds(at, pieces), :] + mm(anom_ref[pl.ds(at, pieces), :], b))
            for t in range(pieces):
                out_ref[r, :, t * wide:(t + 1) * wide] = y_ref[
                    pl.ds(t, cols, stride=pieces), :].astype(BF16)
        return carry

    lax.fori_loop(0, glat, pair_of_rows, 0)


def body(
    ensemble, channel_weights, block_column, innovation, error_precision, block_count, neighbours
):
    rows, cols, row_width = ensemble.shape
    slots = block_column.shape[2]
    levels, obs = channel_weights.shape[3:]
    members = row_width // levels
    glat, glon, entries = neighbours.shape
    points = glat * glon
    wide = 2 * members
    pieces = levels // 2
    lines = 16
    size = slots * members + 2 * slots + 16
    order = [(0, h) for h in range(glon)] + [(g, 0) for g in range(1, glat)]
    order += [(g, h) for g in range(1, glat) for h in range(1, glon)]
    spot = {p: (i // 2, i % 2) for i, p in enumerate(order)}
    index = np.array([g * glon + h for g, h in order])

    columns = block_column[0, 0]
    colrow = jnp.broadcast_to(
        jnp.tile(columns.astype(BF16), obs // slots)[None], (16, obs))
    nb = neighbours.reshape(points * entries)
    ahead = lax.ppermute(nb, "lon", ring("lon", -1, True))
    behind = lax.ppermute(nb, "lon", ring("lon", 1, True))

    anom, cent, pack = pl.pallas_call(
        functools.partial(prepare_kernel, (rows, cols, members, levels, slots, obs)),
        out_shape=(
            jax.ShapeDtypeStruct((rows * cols * pieces, wide), BF16),
            jax.ShapeDtypeStruct((rows * cols * pieces, wide), F32),
            jax.ShapeDtypeStruct((size, obs), BF16),
        ),
        in_specs=[SMEM, SMEM, VMEM, VMEM, VMEM, VMEM, VMEM],
        out_specs=(VMEM, VMEM, VMEM),
        scratch_shapes=[
            pltpu.VMEM((rows * cols * pieces, wide), F32),
            pltpu.VMEM((slots * levels, obs), F32),
        ],
        compiler_params=pltpu.CompilerParams(vmem_limit_bytes=16 << 20),
        name="prepare",
    )(columns, block_count[0], ensemble, channel_weights.reshape(slots * levels, obs),
      innovation[0, 0], error_precision[0, 0], colrow)

    low = lax.ppermute(pack, "lat", ring("lat", 1, False))
    high = lax.ppermute(pack, "lat", ring("lat", -1, False))

    lists = jnp.stack([ahead, behind, nb]).reshape(3, points, entries)[:, index]
    offset = lists // slots
    wanted = jnp.array([-1, 1, 0], jnp.int32)[:, None, None]
    match = offset % 3 - 1 == wanted
    slot = jnp.where(match, offset // 3 * slots + lists % slots, 0)
    starts = (slot // slots) * size + (slot % slots) * members
    padded = jnp.pad(jnp.where(match, slot, -1), ((0, 0), (0, 0), (0, lines - entries)),
                     constant_values=-1)
    hot = (padded.reshape(3, points * lines, 1) == jnp.arange(obs)).astype(F32)

    def gram(targets, which):
        n = len(targets)
        return pl.pallas_call(
            functools.partial(
                gram_kernel,
                (rows, cols, members, slots, obs, entries, size, points, lines), targets, order),
            out_shape=jax.ShapeDtypeStruct((n * points // 4, members + 8, wide), F32),
            in_specs=[SMEM, SMEM, VMEM, ANY, ANY, ANY],
            out_specs=VMEM,
            scratch_shapes=[
                pltpu.VMEM((3 * size, obs), BF16),
                pltpu.VMEM((3 * slots, obs), F32),
                pltpu.VMEM((n * points * lines, obs), F32),
                pltpu.VMEM((2, 2, wide + 16, entries * obs), BF16),
                pltpu.SemaphoreType.DMA((3,)),
            ],
            compiler_params=pltpu.CompilerParams(vmem_limit_bytes=16 << 20),
            cost_estimate=pl.CostEstimate(
                flops=n * points * 2 * (wide + 16) * wide * entries * obs // 2,
                bytes_accessed=3 * size * obs * 2, transcendentals=0),
            name="gram",
        )(starts[which].reshape(-1), slot[which].reshape(-1), hot[which].reshape(-1, obs),
          low, pack, high)

    sides = gram((1.0, -1.0), slice(0, 2))
    quads = points // 4
    from_left = lax.ppermute(sides[:quads], "lon", ring("lon", 1, True))
    from_right = lax.ppermute(sides[quads:], "lon", ring("lon", -1, True))
    middle = gram((0.0,), slice(2, 3))

    trans = pl.pallas_call(
        functools.partial(newton_kernel, members),
        out_shape=jax.ShapeDtypeStruct((points // 2, members, wide), BF16),
        in_specs=[VMEM, VMEM, VMEM],
        out_specs=VMEM,
        scratch_shapes=[
            pltpu.VMEM((points // 2, members, wide), F32),
            pltpu.VMEM((points // 2, wide), F32),
            pltpu.VMEM((points // 2, wide), F32),
            pltpu.VMEM((points // 2, members, wide), F32),
            pltpu.VMEM((points // 2, wide), F32),
        ] + [pltpu.VMEM((points // 2, members, wide), BF16)] * 6,
        compiler_params=pltpu.CompilerParams(vmem_limit_bytes=16 << 20),
        name="newton",
    )(from_left, middle, from_right)

    below = lax.ppermute(trans[:glon // 2], "lat", ring("lat", -1, False))
    edge = glat // 2
    mine = jnp.concatenate([trans[:1], trans[glon // 2:glon // 2 + edge]], 0)
    beside = lax.ppermute(mine, "lon", ring("lon", -1, True))
    corner = lax.ppermute(below[:1], "lon", ring("lon", -1, True))
    last = (lax.axis_index("lat") == lax.axis_size("lat") - 1).astype(jnp.int32)[None]
    return pl.pallas_call(
        functools.partial(
            analysis_kernel, (rows, cols, members, levels, glat, glon), spot),
        out_shape=jax.ShapeDtypeStruct((rows, cols, row_width), BF16),
        in_specs=[SMEM] + [VMEM] * 6,
        out_specs=VMEM,
        scratch_shapes=[
            pltpu.VMEM(((glat + 1) * (glon + 1), members, wide), F32),
            pltpu.VMEM((cols * pieces, wide), F32),
        ],
        compiler_params=pltpu.CompilerParams(vmem_limit_bytes=16 << 20),
        name="analysis",
    )(last, trans, below, beside, corner, anom, cent)


def solution(mesh):
    return jax.shard_map(
        body,
        mesh=mesh,
        in_specs=(
            P("lat", "lon", None),
            P("lat", "lon", None, None, None),
            P("lat", "lon", None),
            P("lat", "lon", None, None),
            P("lat", "lon", None, None),
            P("lat", "lon"),
            P("lat", "lon", None),
        ),
        out_specs=P("lat", "lon", None),
        check_vma=False,
    )
```

time: 208 us -> 61.3 us (0.29)
  waiting for transfers between devices: 73.6 us -> 11.3 us
  local copies, waits for them, and re-layouts: 60.9 us -> 5.72 us
  matrix products: 40 us -> 0 us
  Pallas kernels: 0 us -> 21.6 us
  other arithmetic: 10.3 us -> 0.74 us
  loops' own time: 3.75 us -> 0 us
  starting transfers between devices: 17.8 us -> 20.4 us
    ppermute x6 -> x9, waiting for transfers between devices: 73.6 us -> 11.3 us  [the longest x1 6.21 us: body(): from_right = lax.ppermute(sides[quads:], 'lon', ring('lon', -1, True))]
    dot_general x86 -> x0, matrix products: 40 us -> none  [the longest x24 9.58 us: newton_schulz(): jnp.einsum('pij,pjk->pik', inverse, current, precision=lax.Precision.HIGH...]
    gather x33 -> x1, local copies, waits for them, and re-layouts: 34.7 us -> 0.61 us  [body(): lists = jnp.stack([ahead, behind, nb]).reshape(3, points, entries)[:, index]]
    pallas_call x0 -> x5, Pallas kernels: none -> 21.6 us  [the longest x2 11.4 us: gram(): pl.pallas_call(functools.partial(gram_kernel, (rows, cols, members, slots...]
    slice x5 -> x11, local copies, waits for them, and re-layouts: 7.42 us -> 0.23 us  [the longest x3 0.12 us: gram(): slot[which].reshape(-1)]
    concatenate x11 -> x1, other arithmetic: 4.78 us -> 0.01 us  [body(): mine = jnp.concatenate([trans[:1], trans[glon // 2:glon // 2 + edge]], 0)]
    ppermute x4 -> x0, local copies, waits for them, and re-layouts: 4.62 us -> none  [the longest x2 2.31 us: padded(): lax.ppermute(lax.slice_in_dim(block, 0, width, axis=dim), axis, backward)]
    another operation x1 -> x0, loops' own time: 3.75 us -> none  [body(): lax.map(coarse_row, (jnp.arange(coarse_lat, dtype=jnp.int32), neighbours))]
  transfers between devices with their start and end apart: 6 -> 9, of which waited for: 6 -> 5; matrix products, arithmetic and copies ran while one was open for 2% -> 4% of each run, Pallas kernels for 0% -> 10%
where the time goes in v1:
time: 61.3 us; the launch traced here: 60.8 us
  Pallas kernels  21.6 us (35%)
  starting transfers between devices  20.4 us (33%)
  waiting for transfers between devices  11.3 us (18%)
  local copies, waits for them, and re-layouts  5.72 us (9%)
  between operations  0.97 us (2%)
  other arithmetic  0.74 us (1%)
    pallas_call x2, Pallas kernels, gram(): pl.pallas_call(functools.partial(gram_kernel, (rows, cols, members, slots...  11.4 us
    ppermute x1, waiting for transfers between devices, body(): from_right = lax.ppermute(sides[quads:], 'lon', ring('lon', -1, True))  6.21 us
    pallas_call x1, Pallas kernels, body(): pl.pallas_call(functools.partial(newton_kernel, members), out_shape=jax.S...  5.72 us
    unnamed x17, local copies, waits for them, and re-layouts  3.26 us
    ppermute x1, starting transfers between devices, body(): low = lax.ppermute(pack, 'lat', ring('lat', 1, False))  3.17 us
    ppermute x1, starting transfers between devices, body(): ahead = lax.ppermute(nb, 'lon', ring('lon', -1, True))  3.1 us
    ppermute x1, starting transfers between devices, body(): corner = lax.ppermute(below[:1], 'lon', ring('lon', -1, True))  2.95 us
    ppermute x1, starting transfers between devices, body(): high = lax.ppermute(pack, 'lat', ring('lat', -1, False))  2.86 us
  transfers between devices with their start and end apart: 9, of which 5 were waited for; matrix products, arithmetic and copies ran while one was open for 4% of the time, Pallas kernels for 10%

profile of v1, /device:TPU:1, one launch (start us, length us, event | category | flops | bytes accessed | tf_op | source)
XLA Modules:
  0.0 60.8 jit_solution(2487326012685598283)
XLA Ops:
  0.0 0.8 %reshape.40 = s32[384]{0:T(512)S(1)} reshape(s32[4,8,12]{2,1,0:T(8,128)} %param.16) | data formatting | bytes 3072 | tf_op jit(solution)/shard_map/reshape | solution.py:359
  0.8 0.0 copy-start.4
  0.8 2.1 %collective-permute-start.1 = (s32[384]{0:T(512)S(1)}, s32[384]{0:T(512)S(1)}, u32[]{:S(2)}, u32[]{:S(2)}) collective-permute-start(s32[384]{0:T(512)S(1)} %reshape.40), channel_id=1, source_target_pairs={{0,1},{1,2},{2,3},{3,4},{4,5},{5,6},{6,7},{7,0},{8,9},{9,10},{10,1... | collective-permute-start | bytes 4616 | tf_op jit(solution)/shard_map/ppermute | solution.py:361
  2.9 3.1 %collective-permute-start = (s32[384]{0:T(512)S(1)}, s32[384]{0:T(512)S(1)}, u32[]{:S(2)}, u32[]{:S(2)}) collective-permute-start(s32[384]{0:T(512)S(1)} %reshape.40), channel_id=1, source_target_pairs={{0,7},{1,0},{2,1},{3,2},{4,3},{5,4},{6,5},{7,6},{8,15},{9,8},{10,9... | collective-permute-start | bytes 4616 | tf_op jit(solution)/shard_map/ppermute | solution.py:360
  6.7 0.0 copy-start.3
  6.7 0.0 copy-start.2
  6.7 0.1 broadcast_in_dim.23
  6.8 0.6 copy-done.3
  7.4 0.0 copy-done.2
  7.4 1.0 %copy-done = bf16[8,16,2048]{2,1,0:T(8,128)(2,1)S(1)} copy-done((bf16[8,16,2048]{2,1,0:T(8,128)(2,1)S(1)}, bf16[8,16,2048]{2,1,0:T(8,128)(2,1)}, u32[]{:S(2)}) %copy-start) | copy-done | bytes 524312
  8.5 0.9 %copy-done.1 = bf16[1,1,32,32,128]{4,3,2,1,0:T(8,128)(2,1)S(1)} copy-done((bf16[1,1,32,32,128]{4,3,2,1,0:T(8,128)(2,1)S(1)}, bf16[1,1,32,32,128]{4,3,2,1,0:T(8,128)(2,1)}, u32[]{:S(2)}) %copy-start.1) | copy-done | bytes 262168
  9.4 1.7 %prepare.1 = (bf16[2048,128]{1,0:T(8,128)(2,1)S(1)}, f32[2048,128]{1,0:T(8,128)S(1)}, bf16[2128,128]{1,0:T(8,128)(2,1)S(1)}) custom-call(s32[32]{0:T(128)S(1)} %bitcast.47, s32[1]{0:T(128)} %bitcast.42.count_ref, bf16[8,16,2048]{2,1,0:T(8,128)(2,1)S(1)} %copy-done, bf16[1024,128]{1,0:T(8,128)(2,1)S(1)} %bitcast.44, bf16[32,128]{1,0:T(8,128)(2,1)S(1)} %bitcast.45, ...), custom_call_target="tpu_custom_call" | custom-call | tf_op jit(solution)/shard_map/prepare/pallas_call | solution.py:363
  11.1 0.0 copy-start.7
  11.2 2.9 %collective-permute-start.3 = (bf16[2128,128]{1,0:T(8,128)(2,1)S(1)}, bf16[2128,128]{1,0:T(8,128)(2,1)S(1)}, u32[]{:S(2)}, u32[]{:S(2)}) collective-permute-start(bf16[2128,128]{1,0:T(8,128)(2,1)S(1)} %get-tuple-element.8.own_ref), channel_id=1, source_target_pairs={{8,0},{16,8},{24,16},{9,1},{17,9},{25,17},{10,2},{18,10},{26,18},{... | collective-permute-start | bytes 1634312 | tf_op jit(solution)/shard_map/ppermute | solution.py:382
  14.0 3.2 %collective-permute-start.2 = (bf16[2128,128]{1,0:T(8,128)(2,1)S(1)}, bf16[2128,128]{1,0:T(8,128)(2,1)S(1)}, u32[]{:S(2)}, u32[]{:S(2)}) collective-permute-start(bf16[2128,128]{1,0:T(8,128)(2,1)S(1)} %get-tuple-element.8.own_ref), channel_id=1, source_target_pairs={{0,8},{8,16},{16,24},{1,9},{9,17},{17,25},{2,10},{10,18},{18,26},{... | collective-permute-start | bytes 1634312 | tf_op jit(solution)/shard_map/ppermute | solution.py:381
  17.2 0.1 stack.11
  17.3 0.0 copy-start.5
  17.4 0.0 collective-permute-done.1
  17.4 0.1 stack.12
  17.5 0.6 copy-done.5
  18.1 0.1 pad_add_fusion
  18.1 0.0 copy-start.6
  18.1 0.6 gather_fusion
  18.7 0.0 copy-done.6
  18.8 0.3 broadcast_select_fusion
  19.1 0.1 eq.33
  19.2 0.1 reshape.42.inrow_ref
  19.3 0.1 fusion.6
  19.5 0.1 reshape.41.base_ref
  19.6 0.1 slice_reduce_fusion
  19.7 0.1 reshape.46.inrow_ref
  19.8 0.1 reshape.45.base_ref
  19.9 0.3 fusion
  20.2 2.1 %collective-permute-done.3.high_ref = bf16[2128,128]{1,0:T(8,128)(2,1)S(1)} collective-permute-done((bf16[2128,128]{1,0:T(8,128)(2,1)S(1)}, bf16[2128,128]{1,0:T(8,128)(2,1)S(1)}, u32[]{:S(2)}, u32[]{:S(2)}) %collective-permute-start.3) | collective-permute-done | bytes 544800 | tf_op jit(solution)/shard_map/ppermute | solution.py:382
  22.3 1.2 %collective-permute-done.2.low_ref = bf16[2128,128]{1,0:T(8,128)(2,1)S(1)} collective-permute-done((bf16[2128,128]{1,0:T(8,128)(2,1)S(1)}, bf16[2128,128]{1,0:T(8,128)(2,1)S(1)}, u32[]{:S(2)}, u32[]{:S(2)}) %collective-permute-start.2) | collective-permute-done | bytes 544800 | tf_op jit(solution)/shard_map/ppermute | solution.py:381
  23.5 7.3 %gram.2 = f32[16,72,128]{2,1,0:T(8,128)S(1)} custom-call(s32[768]{0:T(1024)S(1)} %reshape.41.base_ref, s32[768]{0:T(1024)S(1)} %reshape.42.inrow_ref, f32[1024,128]{1,0:T(8,128)S(1)} %bitcast.43, bf16[2128,128]{1,0:T(8,128)(2,1)S(1)} %collective-permute-done.2.low_ref, bf16[2128,128]{1,0:T(8,128)(2,1)S(1)} %get-tuple-element.8.own_ref, ...), custom_call_target="tpu_custom_call" | custom-call | flops 1811939328 | bytes 1634304 | tf_op jit(solution)/shard_map/gram/pallas_call | solution.py:396
  30.9 1.6 %collective-permute-start.5 = (f32[8,72,128]{2,1,0:T(8,128)S(1)}, f32[8,72,128]{2,1,0:T(8,128)S(1)}, u32[]{:S(2)}, u32[]{:S(2)}) collective-permute-start(f32[8,72,128]{2,1,0:T(8,128)S(1)} %get-tuple-element.13), channel_id=1, source_target_pairs={{0,7},{1,0},{2,1},{3,2},{4,3},{5,4},{6,5},{7,6},{8,15},{9,8},{10,9... | collective-permute-start | bytes 884744 | tf_op jit(solution)/shard_map/ppermute | solution.py:421
  32.4 0.0 collective-permute-start.4
  32.5 4.1 %gram.3.own_ref = f32[8,72,128]{2,1,0:T(8,128)S(1)} custom-call(s32[384]{0:T(512)S(1)} %reshape.45.base_ref, s32[384]{0:T(512)S(1)} %reshape.46.inrow_ref, f32[512,128]{1,0:T(8,128)S(1)} %slice_bitcast_fusion.hot_ref, bf16[2128,128]{1,0:T(8,128)(2,1)S(1)} %collective-permute-done.2.low_ref, bf16[2128,128]{1,0:T(8,128)(2,1)S(1)} %get-tuple-element.8.own_ref, ...), custom_call_target="tpu_custom_call" | custom-call | flops 905969664 | bytes 1634304 | tf_op jit(solution)/shard_map/gram/pallas_call | solution.py:396
  36.6 6.2 %collective-permute-done.5.right_ref = f32[8,72,128]{2,1,0:T(8,128)S(1)} collective-permute-done((f32[8,72,128]{2,1,0:T(8,128)S(1)}, f32[8,72,128]{2,1,0:T(8,128)S(1)}, u32[]{:S(2)}, u32[]{:S(2)}) %collective-permute-start.5) | collective-permute-done | bytes 294944 | tf_op jit(solution)/shard_map/ppermute | solution.py:421
  42.8 0.0 collective-permute-done.4.left_ref
  42.8 5.7 %newton.1.own_ref = bf16[16,64,128]{2,1,0:T(8,128)(2,1)S(1)} custom-call(f32[8,72,128]{2,1,0:T(8,128)S(1)} %collective-permute-done.4.left_ref, f32[8,72,128]{2,1,0:T(8,128)S(1)} %gram.3.own_ref, f32[8,72,128]{2,1,0:T(8,128)S(1)} %collective-permute-done.5.right_ref), custom_call_target="tpu_custom_call" | custom-call | tf_op jit(solution)/shard_map/newton/pallas_call | solution.py:424
  48.6 1.9 %collective-permute-start.6 = (bf16[4,64,128]{2,1,0:T(8,128)(2,1)S(1)}, bf16[4,64,128]{2,1,0:T(8,128)(2,1)S(1)}, u32[]{:S(2)}, u32[]{:S(2)}) collective-permute-start(bf16[4,64,128]{2,1,0:T(8,128)(2,1)S(1)} %slice.58), channel_id=1, source_target_pairs={{8,0},{16,8},{24,16},{9,1},{17,9},{25,17},{10,2},{18,10},{26,18},{... | collective-permute-start | bytes 196616 | tf_op jit(solution)/shard_map/ppermute | solution.py:440
  50.5 2.8 %collective-permute-start.7 = (bf16[3,64,128]{2,1,0:T(8,128)(2,1)S(1)}, bf16[3,64,128]{2,1,0:T(8,128)(2,1)S(1)}, u32[]{:S(2)}, u32[]{:S(2)}) collective-permute-start(bf16[3,64,128]{2,1,0:T(8,128)(2,1)S(1)} %pad_maximum_fusion), channel_id=1, source_target_pairs={{0,7},{1,0},{2,1},{3,2},{4,3},{5,4},{6,5},{7,6},{8,15},{9,8},{10,9... | collective-permute-start | bytes 147464 | tf_op jit(solution)/shard_map/ppermute | solution.py:443
  53.3 0.9 %collective-permute-done.6.below_ref = bf16[4,64,128]{2,1,0:T(8,128)(2,1)S(1)} collective-permute-done((bf16[4,64,128]{2,1,0:T(8,128)(2,1)S(1)}, bf16[4,64,128]{2,1,0:T(8,128)(2,1)S(1)}, u32[]{:S(2)}, u32[]{:S(2)}) %collective-permute-start.6) | collective-permute-done | bytes 65568 | tf_op jit(solution)/shard_map/ppermute | solution.py:440
  54.2 2.9 %collective-permute-start.8 = (bf16[1,64,128]{2,1,0:T(8,128)(2,1)S(1)}, bf16[1,64,128]{2,1,0:T(8,128)(2,1)S(1)}, u32[]{:S(2)}, u32[]{:S(2)}) collective-permute-start(bf16[1,64,128]{2,1,0:T(8,128)(2,1)S(1)} %slice.61), channel_id=1, source_target_pairs={{0,7},{1,0},{2,1},{3,2},{4,3},{5,4},{6,5},{7,6},{8,15},{9,8},{10,9... | collective-permute-start | bytes 49160 | tf_op jit(solution)/shard_map/ppermute | solution.py:444
  57.2 0.9 %collective-permute-done.8.corner_ref = bf16[1,64,128]{2,1,0:T(8,128)(2,1)S(1)} collective-permute-done((bf16[1,64,128]{2,1,0:T(8,128)(2,1)S(1)}, bf16[1,64,128]{2,1,0:T(8,128)(2,1)S(1)}, u32[]{:S(2)}, u32[]{:S(2)}) %collective-permute-start.8) | collective-permute-done | bytes 16416 | tf_op jit(solution)/shard_map/ppermute | solution.py:444
  58.0 2.8 %analysis.1 = bf16[8,16,2048]{2,1,0:T(8,128)(2,1)} custom-call(s32[1]{0:T(128)} %bitcast.last_ref, bf16[16,64,128]{2,1,0:T(8,128)(2,1)S(1)} %newton.1.own_ref, bf16[4,64,128]{2,1,0:T(8,128)(2,1)S(1)} %collective-permute-done.6.below_ref, bf16[3,64,128]{2,1,0:T(8,128)(2,1)S(1)} %collective-permute-done.7.beside_ref, ...), custom_call_target="tpu_custom_call" | custom-call | tf_op jit(solution)/shard_map/analysis/pallas_call | solution.py:446
  (24 shorter events, 0.2 us)
Async XLA Ops:
  0.8 5.9 %copy-start.4 = (s32[1,1,32]{2,1,0:T(1,128)S(1)}, s32[1,1,32]{2,1,0:T(1,128)}, u32[]{:S(2)}) copy-start(s32[1,1,32]{2,1,0:T(1,128)} %param.12) | copy-start | bytes 388
  0.8 16.5 %collective-permute-start.1 = (s32[384]{0:T(512)S(1)}, s32[384]{0:T(512)S(1)}, u32[]{:S(2)}, u32[]{:S(2)}) collective-permute-start(s32[384]{0:T(512)S(1)} %reshape.40), channel_id=1, source_target_pairs={{0,1},{1,2},{2,3},{3,4},{4,5},{5,6},{6,7},{7,0},{8,9},{9,10},{10,1... | collective-permute-start | bytes 4616 | tf_op jit(solution)/shard_map/ppermute | solution.py:361
  2.9 14.3 %collective-permute-start = (s32[384]{0:T(512)S(1)}, s32[384]{0:T(512)S(1)}, u32[]{:S(2)}, u32[]{:S(2)}) collective-permute-start(s32[384]{0:T(512)S(1)} %reshape.40), channel_id=1, source_target_pairs={{0,7},{1,0},{2,1},{3,2},{4,3},{5,4},{6,5},{7,6},{8,15},{9,8},{10,9... | collective-permute-start | bytes 4616 | tf_op jit(solution)/shard_map/ppermute | solution.py:360
  6.7 0.7 %copy-start.3 = (bf16[1,1,32,128]{3,2,1,0:T(8,128)(2,1)S(1)}, bf16[1,1,32,128]{3,2,1,0:T(8,128)(2,1)}, u32[]{:S(2)}) copy-start(bf16[1,1,32,128]{3,2,1,0:T(8,128)(2,1)} %param.14) | copy-start | bytes 24580
  6.7 0.7 %copy-start.2 = (bf16[1,1,32,128]{3,2,1,0:T(8,128)(2,1)S(1)}, bf16[1,1,32,128]{3,2,1,0:T(8,128)(2,1)}, u32[]{:S(2)}) copy-start(bf16[1,1,32,128]{3,2,1,0:T(8,128)(2,1)} %param.13) | copy-start | bytes 24580
  7.4 1.0 %copy-start = (bf16[8,16,2048]{2,1,0:T(8,128)(2,1)S(1)}, bf16[8,16,2048]{2,1,0:T(8,128)(2,1)}, u32[]{:S(2)}) copy-start(bf16[8,16,2048]{2,1,0:T(8,128)(2,1)} %ens_ref.1) | copy-start | bytes 1572868
  8.5 0.9 %copy-start.1 = (bf16[1,1,32,32,128]{4,3,2,1,0:T(8,128)(2,1)S(1)}, bf16[1,1,32,32,128]{4,3,2,1,0:T(8,128)(2,1)}, u32[]{:S(2)}) copy-start(bf16[1,1,32,32,128]{4,3,2,1,0:T(8,128)(2,1)} %param.11) | copy-start | bytes 786436
  11.1 6.1 %copy-start.7 = (s32[32]{0:T(128)S(1)}, s32[32]{0:T(128)}, u32[]{:S(2)}) copy-start(s32[32]{0:T(128)} %constant.84) | copy-start | bytes 388
  11.2 11.2 %collective-permute-start.3 = (bf16[2128,128]{1,0:T(8,128)(2,1)S(1)}, bf16[2128,128]{1,0:T(8,128)(2,1)S(1)}, u32[]{:S(2)}, u32[]{:S(2)}) collective-permute-start(bf16[2128,128]{1,0:T(8,128)(2,1)S(1)} %get-tuple-element.8.own_ref), channel_id=1, source_target_pairs={{8,0},{16,8},{24,16},{9,1},{17,9},{25,17},{10,2},{18,10},{26,18},{... | collective-permute-start | bytes 1634312 | tf_op jit(solution)/shard_map/ppermute | solution.py:382
  14.0 9.5 %collective-permute-start.2 = (bf16[2128,128]{1,0:T(8,128)(2,1)S(1)}, bf16[2128,128]{1,0:T(8,128)(2,1)S(1)}, u32[]{:S(2)}, u32[]{:S(2)}) collective-permute-start(bf16[2128,128]{1,0:T(8,128)(2,1)S(1)} %get-tuple-element.8.own_ref), channel_id=1, source_target_pairs={{0,8},{8,16},{16,24},{1,9},{9,17},{17,25},{2,10},{10,18},{18,26},{... | collective-permute-start | bytes 1634312 | tf_op jit(solution)/shard_map/ppermute | solution.py:381
  17.3 0.7 %copy-start.5 = (s32[4,8,12]{2,1,0:T(8,128)S(1)}, s32[4,8,12]{2,1,0:T(8,128)}, u32[]{:S(2)}) copy-start(s32[4,8,12]{2,1,0:T(8,128)} %param.16) | copy-start | bytes 4612
  18.1 0.7 %copy-start.6 = (s32[3]{0:T(128)S(1)}, s32[3]{0:T(128)}, u32[]{:S(2)}) copy-start(s32[3]{0:T(128)} %constant.75.clone) | copy-start | bytes 40
  30.9 11.9 %collective-permute-start.5 = (f32[8,72,128]{2,1,0:T(8,128)S(1)}, f32[8,72,128]{2,1,0:T(8,128)S(1)}, u32[]{:S(2)}, u32[]{:S(2)}) collective-permute-start(f32[8,72,128]{2,1,0:T(8,128)S(1)} %get-tuple-element.13), channel_id=1, source_target_pairs={{0,7},{1,0},{2,1},{3,2},{4,3},{5,4},{6,5},{7,6},{8,15},{9,8},{10,9... | collective-permute-start | bytes 884744 | tf_op jit(solution)/shard_map/ppermute | solution.py:421
  32.4 10.4 %collective-permute-start.4 = (f32[8,72,128]{2,1,0:T(8,128)S(1)}, f32[8,72,128]{2,1,0:T(8,128)S(1)}, u32[]{:S(2)}, u32[]{:S(2)}) collective-permute-start(f32[8,72,128]{2,1,0:T(8,128)S(1)} %get-tuple-element.14), channel_id=1, source_target_pairs={{0,1},{1,2},{2,3},{3,4},{4,5},{5,6},{6,7},{7,0},{8,9},{9,10},{10,1... | collective-permute-start | bytes 884744 | tf_op jit(solution)/shard_map/ppermute | solution.py:420
  48.6 5.6 %collective-permute-start.6 = (bf16[4,64,128]{2,1,0:T(8,128)(2,1)S(1)}, bf16[4,64,128]{2,1,0:T(8,128)(2,1)S(1)}, u32[]{:S(2)}, u32[]{:S(2)}) collective-permute-start(bf16[4,64,128]{2,1,0:T(8,128)(2,1)S(1)} %slice.58), channel_id=1, source_target_pairs={{8,0},{16,8},{24,16},{9,1},{17,9},{25,17},{10,2},{18,10},{26,18},{... | collective-permute-start | bytes 196616 | tf_op jit(solution)/shard_map/ppermute | solution.py:440
  50.5 6.7 %collective-permute-start.7 = (bf16[3,64,128]{2,1,0:T(8,128)(2,1)S(1)}, bf16[3,64,128]{2,1,0:T(8,128)(2,1)S(1)}, u32[]{:S(2)}, u32[]{:S(2)}) collective-permute-start(bf16[3,64,128]{2,1,0:T(8,128)(2,1)S(1)} %pad_maximum_fusion), channel_id=1, source_target_pairs={{0,7},{1,0},{2,1},{3,2},{4,3},{5,4},{6,5},{7,6},{8,15},{9,8},{10,9... | collective-permute-start | bytes 147464 | tf_op jit(solution)/shard_map/ppermute | solution.py:443
  54.2 3.8 %collective-permute-start.8 = (bf16[1,64,128]{2,1,0:T(8,128)(2,1)S(1)}, bf16[1,64,128]{2,1,0:T(8,128)(2,1)S(1)}, u32[]{:S(2)}, u32[]{:S(2)}) collective-permute-start(bf16[1,64,128]{2,1,0:T(8,128)(2,1)S(1)} %slice.61), channel_id=1, source_target_pairs={{0,7},{1,0},{2,1},{3,2},{4,3},{5,4},{6,5},{7,6},{8,15},{9,8},{10,9... | collective-permute-start | bytes 49160 | tf_op jit(solution)/shard_map/ppermute | solution.py:444
